TPU v7x, 32 devices: a whole 2x2x4 slice. The times are simulated.
32 devices in a mesh: grp: 4 (over y, x), dev: 8 (over z, core).
Axes of the slice: x: 2, y: 2, z: 4, core: 2. Of those that a mesh axis runs over, the one named last changes fastest.
Arguments:
- obs_coord: float32 [3, 131072], P(None, ('grp', 'dev')), may hold values from -1 to 1
- obs_resid: float32 [131072], P(('grp', 'dev')), may hold values from -6 to 6
- obs_weight: float32 [131072], P(('grp', 'dev')), may hold values from 0.5 to 2
- obs_dest: int32 [131072], P(('grp', 'dev')), may hold values from 0 to 7, as said below
- obs_send_slot: int32 [131072], P(('grp', 'dev')), may hold values from 0 to 1023, as said below
- obs_elem: int32 [131072], P(('grp', 'dev')), may hold values from 0 to 255, as said below
- obs_slot: int32 [131072], P(('grp', 'dev')), may hold values from 0 to 31, as said below
Outputs:
- nodal: float32 [16, 64, 8, 512], P('grp', 'dev')
- total_cost: float32 [], replicated
Inputs may be any that keep to these rules, and one draw needn't show every extreme that they name: `obs_dest`: from the rows of one device, at most 1024 observations go to any one destination; in every group one destination receives exactly 1024 from every device of the group. `obs_send_slot`: distinct among the rows of one device with the same obs_dest. `obs_elem`: together with obs_slot distinct among all observations of a group with the same obs_dest. `obs_slot`: on every destination some element uses all 32 slots.
All inputs are finite; a program needn't handle non-finite values.
Results may differ from a plain program's by a relative error of at most 0.00017.
Values sent between devices are 32-bit elements; how exact they have to be, the bound alone decides.
A program may use at most 64 MiB of HBM per device.

v0:
```python
import math
import jax
import jax.numpy as jnp
from jax import lax
from jax.sharding import PartitionSpec as P

EX = 4
EY = 8
EZ = 8
ELEM_DEV = 256
SLOTS = 32


def with_halo(block, sides, width):
    for axis, dim in sides:
        count = lax.axis_size(axis)
        forward = [(i, i + 1) for i in range(count - 1)]
        backward = [(target, source) for source, target in forward]
        low = lax.ppermute(
            lax.slice_in_dim(block, block.shape[dim] - width, None, axis=dim), axis, forward
        )
        high = lax.ppermute(lax.slice_in_dim(block, 0, width, axis=dim), axis, backward)
        block = jnp.concatenate([low, block, high], axis=dim)
    return block


def basis_values(position):
    anchors = [-math.cos(math.pi * k / 7) for k in range(8)]
    basis = []
    for node_i in range(8):
        factor = jnp.ones_like(position)
        for node_m in range(8):
            if node_m != node_i:
                factor = factor * (
                    (position - anchors[node_m]) / (anchors[node_i] - anchors[node_m])
                )
        basis.append(factor)
    return jnp.stack(basis)


def contract(first_w, second_w, third_w):
    outer = (first_w[:, None, :] * second_w[None, :, :]).reshape(64, ELEM_DEV, SLOTS)
    third = third_w.reshape(8, ELEM_DEV, SLOTS)
    mixed = jnp.einsum("aes,kes->eak", outer, third, precision=lax.Precision.HIGHEST)
    return mixed.reshape(ELEM_DEV, 512)


def combine(field, elem_dim, node_dim, from_low, from_high):
    count = field.shape[elem_dim]
    low_plane = lax.slice_in_dim(field, 0, 1, axis=node_dim)
    high_plane = lax.slice_in_dim(field, 7, 8, axis=node_dim)
    after = jnp.concatenate(
        [lax.slice_in_dim(low_plane, 1, count, axis=elem_dim), from_high], axis=elem_dim
    )
    before = jnp.concatenate(
        [from_low, lax.slice_in_dim(high_plane, 0, count - 1, axis=elem_dim)], axis=elem_dim
    )
    middle = lax.slice_in_dim(field, 1, 7, axis=node_dim)
    return jnp.concatenate([low_plane + before, middle, high_plane + after], axis=node_dim)


def boundary(field, elem_dim, node_dim):
    count = field.shape[elem_dim]
    low_plane = lax.slice_in_dim(field, 0, 1, axis=node_dim)
    high_plane = lax.slice_in_dim(field, 7, 8, axis=node_dim)
    return jnp.concatenate(
        [
            lax.slice_in_dim(low_plane, 0, 1, axis=elem_dim),
            lax.slice_in_dim(high_plane, count - 1, count, axis=elem_dim),
        ],
        axis=elem_dim,
    )


def on_device(obs_coord, obs_resid, obs_weight, obs_dest, obs_send_slot, obs_elem, obs_slot):
    peer_count = lax.axis_size("dev")
    row_count = obs_resid.shape[0]
    capacity = 2 * row_count // peer_count
    cell_count = ELEM_DEV * SLOTS
    forcing = obs_weight * obs_resid
    total_cost = lax.psum(0.5 * jnp.sum(forcing * obs_resid), ("grp", "dev"))
    payload = jnp.concatenate([obs_coord, forcing[None, :]], axis=0)
    channels = payload.shape[0]
    target = obs_dest * capacity + obs_send_slot
    cell_ids = obs_elem * SLOTS + obs_slot
    send_values = (
        jnp.zeros((channels, peer_count * capacity), payload.dtype).at[:, target].set(payload)
    )
    send_cells = jnp.full((peer_count * capacity,), cell_count, jnp.int32).at[target].set(cell_ids)
    send_values = send_values.reshape(channels, peer_count, capacity)
    send_cells = send_cells.reshape(1, peer_count, capacity)
    got_values, got_cells = (
        lax.all_to_all(send_values, "dev", split_axis=1, concat_axis=1, tiled=True),
        lax.all_to_all(send_cells, "dev", split_axis=1, concat_axis=1, tiled=True),
    )
    packed = jnp.zeros((channels, cell_count + 1), payload.dtype)
    packed = packed.at[:, got_cells.reshape(-1)].set(got_values.reshape(channels, -1))[
        :, :cell_count
    ]
    first_w = basis_values(packed[0]) * packed[3]
    second_w = basis_values(packed[1])
    third_w = basis_values(packed[2])
    field = contract(first_w, second_w, third_w).reshape(EX, EY, EZ, 8, 8, 8)
    padded = with_halo(boundary(field, 0, 3), (("grp", 0),), 1)
    field = combine(field, 0, 3, padded[0:1], padded[3:4])
    padded = with_halo(boundary(field, 1, 4), (("dev", 1),), 1)
    field = combine(field, 1, 4, padded[:, 0:1], padded[:, 3:4])
    empty = jnp.zeros_like(lax.slice_in_dim(lax.slice_in_dim(field, 0, 1, axis=5), 0, 1, axis=2))
    field = combine(field, 2, 5, empty, empty)
    return (field.reshape(EX, EY, EZ, 512), total_cost)


def solution(mesh):
    placed = (
        P(None, ("grp", "dev")),
        P(("grp", "dev")),
        P(("grp", "dev")),
        P(("grp", "dev")),
        P(("grp", "dev")),
        P(("grp", "dev")),
        P(("grp", "dev")),
    )
    return jax.shard_map(
        on_device,
        mesh=mesh,
        in_specs=placed,
        out_specs=(P("grp", "dev", None, None), P()),
        check_vma=False,
    )
```

profile of v0, /device:TPU:1, one launch (start us, length us, event | category | flops | bytes accessed | tf_op | source)
XLA Modules:
  0.0 226.2 jit_solution(2030563538721729877)
XLA Ops:
  1.4 16.1 %scatter_custom_fusion = s32[8192]{0:T(1024)} fusion(s32[4096]{0:T(1024)S(1)} %get-tuple-element.54, s32[4096]{0:T(1024)S(1)} %get-tuple-element.55, s32[]{:T(128)} %constant.245.clone.1), kind=kCustom, calls=%fused_computation.88 | custom fusion | bytes 32772 | tf_op jit(solution)/shard_map/scatter | solution.py:89
  17.5 6.4 %all-to-all-start = ((s32[1,8,1024]{2,0,1:T(1,128)}), s32[1,8,1024]{2,0,1:T(1,128)S(1)}, u32[]{:S(2)}, u32[]{:S(2)}) async-start(s32[1,8,1024]{2,0,1:T(1,128)} %bitcast), calls=%async_computation | async-start | bytes 65536 | tf_op jit(solution)/shard_map/all_to_all | solution.py:94
  23.9 1.3 multiply_reduce_fusion.8
  26.7 39.5 %psum.7 = f32[]{:T(128)} all-reduce(f32[]{:T(128)S(6)} %mul_shard_map.3), channel_id=1, replica_groups=mesh['grp'=4,'dev'=8] {'grp','dev'}, use_global_device_ids=true, to_apply=%region_4.0 | all-reduce | flops 1 | bytes 8 | tf_op jit(solution)/shard_map/psum | solution.py:81
  66.9 12.8 %scatter_custom_fusion.1 = f32[4,8192]{0,1:T(8,128)} fusion(s32[4096]{0:T(1024)S(1)} %get-tuple-element.54, f32[4096,4]{1,0:T(8,128)S(1)} %copy.404, f32[]{:T(128)} %constant.244.clone.1), kind=kCustom, calls=%fused_computation.11 | custom fusion | bytes 131076 | tf_op jit(solution)/shard_map/scatter | solution.py:87
  79.6 3.5 %copy.405 = f32[4,8,1024]{2,0,1:T(4,128)} copy(f32[4,8,1024]{0,2,1:T(8,128)} %bitcast.26) | data formatting | bytes 262144 | tf_op jit(solution)/shard_map/reshape | solution.py:90
  83.1 4.9 %all-to-all-start.1 = ((f32[4,8,1024]{2,0,1:T(4,128)}), f32[4,8,1024]{2,0,1:T(4,128)S(1)}, u32[]{:S(2)}, u32[]{:S(2)}) async-start(f32[4,8,1024]{2,0,1:T(4,128)} %copy.405), calls=%async_computation.1 | async-start | bytes 262144 | tf_op jit(solution)/shard_map/all_to_all | solution.py:93
  88.0 5.7 %all-to-all-done.1 = f32[4,8,1024]{2,0,1:T(4,128)S(1)} async-done(((f32[4,8,1024]{2,0,1:T(4,128)}), f32[4,8,1024]{2,0,1:T(4,128)S(1)}, u32[]{:S(2)}, u32[]{:S(2)}) %all-to-all-start.1) | async-done | bytes 131104 | tf_op jit(solution)/shard_map/all_to_all | solution.py:93
  93.7 2.6 %copy.406 = f32[8192,4]{1,0:T(8,128)} copy(f32[8192,4]{0,1:T(4,128)S(1)} %bitcast.35) | data formatting | bytes 262144 | tf_op jit(solution)/shard_map/reshape | solution.py:97
  96.4 23.0 %scatter_custom_fusion.2 = f32[4,8193]{0,1:T(8,128)} fusion(s32[8192]{0:T(1024)S(1)} %bitcast.38, f32[8192,4]{1,0:T(8,128)} %copy.406, f32[]{:T(128)} %constant.244.clone.1), kind=kCustom, calls=%fused_computation.9 | custom fusion | bytes 131600 | tf_op jit(solution)/shard_map/scatter | solution.py:97
  119.4 14.8 %slice_reduce_fusion = (f32[8192]{0:T(1024)S(1)}, f32[1,8192]{0,1:T(8,128)}, f32[1,8192]{0,1:T(8,128)}, f32[1,8192]{0,1:T(8,128)}) fusion(f32[4,8193]{0,1:T(8,128)} %scatter_custom_fusion.2), kind=kLoop, calls=%fused_computation.8 | loop fusion | bytes 262144 | tf_op jit(solution)/shard_map/slice | solution.py:100
  134.2 2.8 %copy.422 = f32[1,8192]{1,0:T(1,128)S(1)} copy(f32[1,8192]{0,1:T(8,128)} %get-tuple-element.35) | data formatting | bytes 65536
  137.0 2.8 %copy.421 = f32[1,8192]{1,0:T(1,128)S(1)} copy(f32[1,8192]{0,1:T(8,128)} %get-tuple-element.36) | data formatting | bytes 65536
  139.9 2.8 %copy.423 = f32[1,8192]{1,0:T(1,128)S(1)} copy(f32[1,8192]{0,1:T(8,128)} %get-tuple-element.37) | data formatting | bytes 65536
  142.7 1.9 multiply_reduce_fusion
  149.0 4.8 %mul.732 = f32[64,256,32]{2,1,0:T(8,128)} reshape(f32[8,8,8192]{2,1,0:T(8,128)S(1)} %broadcast_multiply_fusion) | data formatting | bytes 4194304 | tf_op jit(solution)/shard_map/mul | solution.py:42
  153.8 1.6 stack.59
  155.4 20.7 %fusion = f32[256,64,8]{1,2,0:T(8,128)S(1)} fusion(f32[8,256,32]{2,0,1:T(8,128)S(1)} %stack.59, f32[64,256,32]{2,1,0:T(8,128)} %mul.732), kind=kOutput, calls=%fused_computation.6 | convolution fusion | flops 50331648 | bytes 2883584 | tf_op jit(solution)/shard_map/aes,kes->eak/dot_general | solution.py:44
  176.5 6.2 %reshape_reshape.3 = f32[4,8,8,8,8,8]{2,1,0,5,4,3:T(8,128)} reshape(f32[256,64,8]{0,2,1:T(8,128)S(1)} %copy.419) | data formatting | bytes 1048576 | tf_op jit(solution)/shard_map/reshape;reshape | solution.py:103
  183.8 3.9 %collective-permute-start = (f32[1,8,8,1,8,8]{2,1,0,5,4,3:T(8,128)S(1)}, f32[1,8,8,1,8,8]{2,1,0,5,4,3:T(8,128)S(1)}, u32[]{:S(2)}, u32[]{:S(2)}) collective-permute-start(f32[1,8,8,1,8,8]{2,1,0,5,4,3:T(8,128)S(1)} %get-tuple-element.30), channel_id=1, source_target_pairs={{0,8},{8,16},{16,24},{1,9},{9,17},{17,25},{2,10},{10,18},{18,26},{... | collective-permute-start | bytes 49160 | tf_op jit(solution)/shard_map/ppermute | solution.py:19
  187.7 1.3 collective-permute-start.1
  189.0 1.5 fusion.15
  190.5 3.5 %slice.118 = f32[4,8,8,6,8,8]{2,1,0,5,4,3:T(8,128)S(1)} slice(f32[4,8,8,8,8,8]{2,1,0,5,4,3:T(8,128)} %reshape_reshape.3), slice={[0:4], [0:8], [0:8], [1:7], [0:8], [0:8]} | slice | bytes 786432 | tf_op jit(solution)/shard_map/slice | solution.py:58
  194.0 6.1 %collective-permute-done.1 = f32[1,8,8,1,8,8]{2,1,0,5,4,3:T(8,128)S(1)} collective-permute-done((f32[1,8,8,1,8,8]{2,1,0,5,4,3:T(8,128)S(1)}, f32[1,8,8,1,8,8]{2,1,0,5,4,3:T(8,128)S(1)}, u32[]{:S(2)}, u32[]{:S(2)}) %collective-permute-start.1) | collective-permute-done | bytes 16416 | tf_op jit(solution)/shard_map/ppermute | solution.py:22
  200.1 1.9 slice_add_fusion.1
  202.3 4.4 %collective-permute-start.2 = (f32[4,1,8,8,1,8]{2,1,0,5,4,3:T(1,128)S(1)}, f32[4,1,8,8,1,8]{2,1,0,5,4,3:T(1,128)S(1)}, u32[]{:S(2)}, u32[]{:S(2)}) collective-permute-start(f32[4,1,8,8,1,8]{2,1,0,5,4,3:T(1,128)S(1)} %get-tuple-element.26), channel_id=1, source_target_pairs={{0,1},{1,2},{2,3},{3,4},{4,5},{5,6},{6,7},{8,9},{9,10},{10,11},{11... | collective-permute-start | bytes 24584 | tf_op jit(solution)/shard_map/ppermute | solution.py:19
  206.7 1.9 collective-permute-start.3
  208.6 1.9 pad_maximum_fusion
  210.5 1.2 slice.122
  214.1 1.6 pad_maximum_fusion.1
  216.6 3.7 %pad_maximum_fusion.2 = f32[4,8,8,8,8,8]{2,1,0,5,4,3:T(8,128)} fusion(f32[4,8,8,8,8,1]{2,1,0,5,4,3:T(8,128)S(1)} %get-tuple-element.23, f32[4,8,8,8,8,6]{2,1,0,5,4,3:T(8,128)S(1)} %slice.123, f32[4,8,8,8,8,1]{2,1,0,5,4,3:T(8,128)S(1)} %get-tuple-element.22), kind=kLoop, calls=%fused_computation.5 | loop fusion | flops 262144 | bytes 1048576 | tf_op jit(solution)/shard_map/concatenate | solution.py:59
  220.3 5.9 %copy.420 = f32[4,8,8,512]{3,2,1,0:T(8,128)} copy(f32[4,8,8,512]{2,1,0,3:T(8,128)} %bitcast.25) | data formatting | bytes 1048576
  (30 shorter events, 11.6 us)
Async XLA Ops:
  17.5 65.6 %all-to-all-start = ((s32[1,8,1024]{2,0,1:T(1,128)}), s32[1,8,1024]{2,0,1:T(1,128)S(1)}, u32[]{:S(2)}, u32[]{:S(2)}) async-start(s32[1,8,1024]{2,0,1:T(1,128)} %bitcast), calls=%async_computation | async-start | bytes 65536 | tf_op jit(solution)/shard_map/all_to_all | solution.py:94
  83.1 10.6 %all-to-all-start.1 = ((f32[4,8,1024]{2,0,1:T(4,128)}), f32[4,8,1024]{2,0,1:T(4,128)S(1)}, u32[]{:S(2)}, u32[]{:S(2)}) async-start(f32[4,8,1024]{2,0,1:T(4,128)} %copy.405), calls=%async_computation.1 | async-start | bytes 262144 | tf_op jit(solution)/shard_map/all_to_all | solution.py:93
  149.0 4.8 %copy-start = (f32[1,256,32]{2,1,0:T(8,128)S(1)}, f32[1,256,32]{2,1,0:T(8,128)}, u32[]{:S(2)}) copy-start(f32[1,256,32]{2,1,0:T(8,128)} %stack.24) | copy-start | bytes 98308
  183.8 10.2 %collective-permute-start = (f32[1,8,8,1,8,8]{2,1,0,5,4,3:T(8,128)S(1)}, f32[1,8,8,1,8,8]{2,1,0,5,4,3:T(8,128)S(1)}, u32[]{:S(2)}, u32[]{:S(2)}) collective-permute-start(f32[1,8,8,1,8,8]{2,1,0,5,4,3:T(8,128)S(1)} %get-tuple-element.30), channel_id=1, source_target_pairs={{0,8},{8,16},{16,24},{1,9},{9,17},{17,25},{2,10},{10,18},{18,26},{... | collective-permute-start | bytes 49160 | tf_op jit(solution)/shard_map/ppermute | solution.py:19
  187.7 12.4 %collective-permute-start.1 = (f32[1,8,8,1,8,8]{2,1,0,5,4,3:T(8,128)S(1)}, f32[1,8,8,1,8,8]{2,1,0,5,4,3:T(8,128)S(1)}, u32[]{:S(2)}, u32[]{:S(2)}) collective-permute-start(f32[1,8,8,1,8,8]{2,1,0,5,4,3:T(8,128)S(1)} %get-tuple-element.31), channel_id=1, source_target_pairs={{8,0},{16,8},{24,16},{9,1},{17,9},{25,17},{10,2},{18,10},{26,18},{... | collective-permute-start | bytes 49160 | tf_op jit(solution)/shard_map/ppermute | solution.py:22
  202.3 9.4 %collective-permute-start.2 = (f32[4,1,8,8,1,8]{2,1,0,5,4,3:T(1,128)S(1)}, f32[4,1,8,8,1,8]{2,1,0,5,4,3:T(1,128)S(1)}, u32[]{:S(2)}, u32[]{:S(2)}) collective-permute-start(f32[4,1,8,8,1,8]{2,1,0,5,4,3:T(1,128)S(1)} %get-tuple-element.26), channel_id=1, source_target_pairs={{0,1},{1,2},{2,3},{3,4},{4,5},{5,6},{6,7},{8,9},{9,10},{10,11},{11... | collective-permute-start | bytes 24584 | tf_op jit(solution)/shard_map/ppermute | solution.py:19
  206.7 6.3 %collective-permute-start.3 = (f32[4,1,8,8,1,8]{2,1,0,5,4,3:T(1,128)S(1)}, f32[4,1,8,8,1,8]{2,1,0,5,4,3:T(1,128)S(1)}, u32[]{:S(2)}, u32[]{:S(2)}) collective-permute-start(f32[4,1,8,8,1,8]{2,1,0,5,4,3:T(1,128)S(1)} %get-tuple-element.27), channel_id=1, source_target_pairs={{1,0},{2,1},{3,2},{4,3},{5,4},{6,5},{7,6},{9,8},{10,9},{11,10},{12... | collective-permute-start | bytes 24584 | tf_op jit(solution)/shard_map/ppermute | solution.py:22
where the time goes:
time: 227 us; the launch traced here: 226 us
  local copies, waits for them, and re-layouts  111 us (49%)
  blocking collectives  39.5 us (17%)
  starting transfers between devices  22.7 us (10%)
  matrix products  20.7 us (9%)
  other arithmetic  17.6 us (8%)
  waiting for transfers between devices  13 us (6%)
    psum x1, blocking collectives, on_device(): total_cost = lax.psum(0.5 * jnp.sum(forcing * obs_resid), ('grp', 'dev'))  39.5 us
    scatter x1, local copies, waits for them, and re-layouts, on_device(): packed.at[:, got_cells.reshape(-1)].set(got_values.reshape(channels, -1))  23 us
    dot_general x1, matrix products, contract(): jnp.einsum('aes,kes->eak', outer, third, precision=lax.Precision.HIGHEST)  20.7 us
    scatter x1, local copies, waits for them, and re-layouts, on_device(): jnp.full((peer_count * capacity,), cell_count, jnp.int32).at[target]  16.1 us
    slice x1, local copies, waits for them, and re-layouts, on_device(): first_w = basis_values(packed[0]) * packed[3]  14.8 us
    unnamed x6, local copies, waits for them, and re-layouts  14.4 us
    scatter x1, local copies, waits for them, and re-layouts, on_device(): jnp.zeros((channels, peer_count * capacity), payload.dtype).at[:, target]  12.8 us
    ppermute x2, starting transfers between devices, with_halo(): lax.ppermute(lax.slice_in_dim(block, block.shape[dim] - width, None, axis...  8.28 us
  transfers between devices with their start and end apart: 6, of which 3 were waited for; matrix products, arithmetic and copies ran while one was open for 12% of the time, Pallas kernels for 0%

commit v1 on v0

--- a/solution.py
+++ b/solution.py
@@ -78,7 +78,7 @@
     capacity = 2 * row_count // peer_count
     cell_count = ELEM_DEV * SLOTS
     forcing = obs_weight * obs_resid
-    total_cost = lax.psum(0.5 * jnp.sum(forcing * obs_resid), ("grp", "dev"))
+    total_cost = jnp.sum(lax.all_gather(0.5 * jnp.sum(forcing * obs_resid), ("grp", "dev")), axis=0)
     payload = jnp.concatenate([obs_coord, forcing[None, :]], axis=0)
     channels = payload.shape[0]
     target = obs_dest * capacity + obs_send_slot

time: 227 us -> 228 us (level)
    psum x1 -> x0, blocking collectives: 39.5 us -> none  [on_device(): total_cost = lax.psum(0.5 * jnp.sum(forcing * obs_resid), ('grp', 'dev'))]
    unnamed x0 -> x1, blocking collectives: none -> 39.3 us
    unnamed x6 -> x8, local copies, waits for them, and re-layouts: 14.4 us -> 14.5 us
where the time goes in v1:
time: 228 us; the launch traced here: 227 us
  local copies, waits for them, and re-layouts  111 us (49%)
  blocking collectives  39.3 us (17%)
  starting transfers between devices  22.9 us (10%)
  matrix products  20.7 us (9%)
  other arithmetic  18.2 us (8%)
  waiting for transfers between devices  12.8 us (6%)
    unnamed x1, blocking collectives  39.3 us
    scatter x1, local copies, waits for them, and re-layouts, on_device(): packed.at[:, got_cells.reshape(-1)].set(got_values.reshape(channels, -1))  23 us
    dot_general x1, matrix products, contract(): jnp.einsum('aes,kes->eak', outer, third, precision=lax.Precision.HIGHEST)  20.7 us
    scatter x1, local copies, waits for them, and re-layouts, on_device(): jnp.full((peer_count * capacity,), cell_count, jnp.int32).at[target]  16.1 us
    slice x1, local copies, waits for them, and re-layouts, on_device(): first_w = basis_values(packed[0]) * packed[3]  14.8 us
    unnamed x8, local copies, waits for them, and re-layouts  14.5 us
    scatter x1, local copies, waits for them, and re-layouts, on_device(): jnp.zeros((channels, peer_count * capacity), payload.dtype).at[:, target]  12.8 us
    ppermute x2, starting transfers between devices, with_halo(): lax.ppermute(lax.slice_in_dim(block, block.shape[dim] - width, None, axis...  8.28 us
  transfers between devices with their start and end apart: 6, of which 3 were waited for; matrix products, arithmetic and copies ran while one was open for 12% of the time, Pallas kernels for 0%

profile of v1, /device:TPU:1, one launch (start us, length us, event | category | flops | bytes accessed | tf_op | source)
XLA Modules:
  0.0 226.7 jit_solution(345657072784228396)
XLA Ops:
  1.4 16.1 %scatter_custom_fusion = s32[8192]{0:T(1024)} fusion(s32[4096]{0:T(1024)S(1)} %get-tuple-element.54, s32[4096]{0:T(1024)S(1)} %get-tuple-element.55, s32[]{:T(128)} %constant.245.clone.1), kind=kCustom, calls=%fused_computation.88 | custom fusion | bytes 32772 | tf_op jit(solution)/shard_map/scatter | solution.py:89
  17.5 6.4 %all-to-all-start = ((s32[1,8,1024]{2,0,1:T(1,128)}), s32[1,8,1024]{2,0,1:T(1,128)S(1)}, u32[]{:S(2)}, u32[]{:S(2)}) async-start(s32[1,8,1024]{2,0,1:T(1,128)} %bitcast), calls=%async_computation | async-start | bytes 65536 | tf_op jit(solution)/shard_map/all_to_all | solution.py:94
  23.9 1.3 multiply_reduce_fusion.8
  26.9 39.3 %all-reduce.2 = f32[32]{0:T(128)S(1)} all-reduce(f32[32]{0:T(128)S(1)} %dynamic-update-slice), channel_id=1, replica_groups=mesh['grp'=4,'dev'=8] {'grp','dev'}, use_global_device_ids=true, to_apply=%add.2 | all-reduce | flops 32 | bytes 256
  67.4 12.8 %scatter_custom_fusion.1 = f32[4,8192]{0,1:T(8,128)} fusion(s32[4096]{0:T(1024)S(1)} %get-tuple-element.54, f32[4096,4]{1,0:T(8,128)S(1)} %copy.404, f32[]{:T(128)} %constant.244.clone.1), kind=kCustom, calls=%fused_computation.11 | custom fusion | bytes 131076 | tf_op jit(solution)/shard_map/scatter | solution.py:87
  80.2 3.5 %copy.405 = f32[4,8,1024]{2,0,1:T(4,128)} copy(f32[4,8,1024]{0,2,1:T(8,128)} %bitcast.27) | data formatting | bytes 262144 | tf_op jit(solution)/shard_map/reshape | solution.py:90
  83.7 5.0 %all-to-all-start.1 = ((f32[4,8,1024]{2,0,1:T(4,128)}), f32[4,8,1024]{2,0,1:T(4,128)S(1)}, u32[]{:S(2)}, u32[]{:S(2)}) async-start(f32[4,8,1024]{2,0,1:T(4,128)} %copy.405), calls=%async_computation.1 | async-start | bytes 262144 | tf_op jit(solution)/shard_map/all_to_all | solution.py:93
  88.7 5.7 %all-to-all-done.1 = f32[4,8,1024]{2,0,1:T(4,128)S(1)} async-done(((f32[4,8,1024]{2,0,1:T(4,128)}), f32[4,8,1024]{2,0,1:T(4,128)S(1)}, u32[]{:S(2)}, u32[]{:S(2)}) %all-to-all-start.1) | async-done | bytes 131104 | tf_op jit(solution)/shard_map/all_to_all | solution.py:93
  94.5 2.6 %copy.406 = f32[8192,4]{1,0:T(8,128)} copy(f32[8192,4]{0,1:T(4,128)S(1)} %bitcast.36) | data formatting | bytes 262144 | tf_op jit(solution)/shard_map/reshape | solution.py:97
  97.1 23.0 %scatter_custom_fusion.2 = f32[4,8193]{0,1:T(8,128)} fusion(s32[8192]{0:T(1024)S(1)} %bitcast.39, f32[8192,4]{1,0:T(8,128)} %copy.406, f32[]{:T(128)} %constant.244.clone.1), kind=kCustom, calls=%fused_computation.9 | custom fusion | bytes 131600 | tf_op jit(solution)/shard_map/scatter | solution.py:97
  120.1 14.8 %slice_reduce_fusion = (f32[8192]{0:T(1024)S(1)}, f32[1,8192]{0,1:T(8,128)}, f32[1,8192]{0,1:T(8,128)}, f32[1,8192]{0,1:T(8,128)}) fusion(f32[4,8193]{0,1:T(8,128)} %scatter_custom_fusion.2), kind=kLoop, calls=%fused_computation.8 | loop fusion | bytes 262144 | tf_op jit(solution)/shard_map/slice | solution.py:100
  134.9 2.8 %copy.422 = f32[1,8192]{1,0:T(1,128)S(1)} copy(f32[1,8192]{0,1:T(8,128)} %get-tuple-element.35) | data formatting | bytes 65536
  137.8 2.8 %copy.421 = f32[1,8192]{1,0:T(1,128)S(1)} copy(f32[1,8192]{0,1:T(8,128)} %get-tuple-element.36) | data formatting | bytes 65536
  140.6 2.8 %copy.423 = f32[1,8192]{1,0:T(1,128)S(1)} copy(f32[1,8192]{0,1:T(8,128)} %get-tuple-element.37) | data formatting | bytes 65536
  143.5 1.9 multiply_reduce_fusion
  149.7 4.8 %mul.732 = f32[64,256,32]{2,1,0:T(8,128)} reshape(f32[8,8,8192]{2,1,0:T(8,128)S(1)} %broadcast_multiply_fusion) | data formatting | bytes 4194304 | tf_op jit(solution)/shard_map/mul | solution.py:42
  154.5 1.6 stack.59
  156.1 20.7 %fusion = f32[256,64,8]{1,2,0:T(8,128)S(1)} fusion(f32[8,256,32]{2,0,1:T(8,128)S(1)} %stack.59, f32[64,256,32]{2,1,0:T(8,128)} %mul.732), kind=kOutput, calls=%fused_computation.6 | convolution fusion | flops 50331648 | bytes 2883584 | tf_op jit(solution)/shard_map/aes,kes->eak/dot_general | solution.py:44
  177.3 6.2 %reshape_reshape.3 = f32[4,8,8,8,8,8]{2,1,0,5,4,3:T(8,128)} reshape(f32[256,64,8]{0,2,1:T(8,128)S(1)} %copy.419) | data formatting | bytes 1048576 | tf_op jit(solution)/shard_map/reshape;reshape | solution.py:103
  184.5 3.9 %collective-permute-start = (f32[1,8,8,1,8,8]{2,1,0,5,4,3:T(8,128)S(1)}, f32[1,8,8,1,8,8]{2,1,0,5,4,3:T(8,128)S(1)}, u32[]{:S(2)}, u32[]{:S(2)}) collective-permute-start(f32[1,8,8,1,8,8]{2,1,0,5,4,3:T(8,128)S(1)} %get-tuple-element.30), channel_id=1, source_target_pairs={{0,8},{8,16},{16,24},{1,9},{9,17},{17,25},{2,10},{10,18},{18,26},{... | collective-permute-start | bytes 49160 | tf_op jit(solution)/shard_map/ppermute | solution.py:19
  188.4 1.3 collective-permute-start.1
  189.7 1.5 fusion.15
  191.2 3.5 %slice.118 = f32[4,8,8,6,8,8]{2,1,0,5,4,3:T(8,128)S(1)} slice(f32[4,8,8,8,8,8]{2,1,0,5,4,3:T(8,128)} %reshape_reshape.3), slice={[0:4], [0:8], [0:8], [1:7], [0:8], [0:8]} | slice | bytes 786432 | tf_op jit(solution)/shard_map/slice | solution.py:58
  194.7 5.9 %collective-permute-done.1 = f32[1,8,8,1,8,8]{2,1,0,5,4,3:T(8,128)S(1)} collective-permute-done((f32[1,8,8,1,8,8]{2,1,0,5,4,3:T(8,128)S(1)}, f32[1,8,8,1,8,8]{2,1,0,5,4,3:T(8,128)S(1)}, u32[]{:S(2)}, u32[]{:S(2)}) %collective-permute-start.1) | collective-permute-done | bytes 16416 | tf_op jit(solution)/shard_map/ppermute | solution.py:22
  200.6 1.9 slice_add_fusion.1
  202.9 4.4 %collective-permute-start.2 = (f32[4,1,8,8,1,8]{2,1,0,5,4,3:T(1,128)S(1)}, f32[4,1,8,8,1,8]{2,1,0,5,4,3:T(1,128)S(1)}, u32[]{:S(2)}, u32[]{:S(2)}) collective-permute-start(f32[4,1,8,8,1,8]{2,1,0,5,4,3:T(1,128)S(1)} %get-tuple-element.26), channel_id=1, source_target_pairs={{0,1},{1,2},{2,3},{3,4},{4,5},{5,6},{6,7},{8,9},{9,10},{10,11},{11... | collective-permute-start | bytes 24584 | tf_op jit(solution)/shard_map/ppermute | solution.py:19
  207.2 1.9 collective-permute-start.3
  209.1 1.9 pad_maximum_fusion
  211.0 1.2 slice.122
  214.7 1.6 pad_maximum_fusion.1
  217.1 3.7 %pad_maximum_fusion.2 = f32[4,8,8,8,8,8]{2,1,0,5,4,3:T(8,128)} fusion(f32[4,8,8,8,8,1]{2,1,0,5,4,3:T(8,128)S(1)} %get-tuple-element.23, f32[4,8,8,8,8,6]{2,1,0,5,4,3:T(8,128)S(1)} %slice.123, f32[4,8,8,8,8,1]{2,1,0,5,4,3:T(8,128)S(1)} %get-tuple-element.22), kind=kLoop, calls=%fused_computation.5 | loop fusion | flops 262144 | bytes 1048576 | tf_op jit(solution)/shard_map/concatenate | solution.py:59
  220.8 5.9 %copy.420 = f32[4,8,8,512]{3,2,1,0:T(8,128)} copy(f32[4,8,8,512]{2,1,0,3:T(8,128)} %bitcast.26) | data formatting | bytes 1048576
  (33 shorter events, 12.3 us)
Async XLA Ops:
  17.5 66.2 %all-to-all-start = ((s32[1,8,1024]{2,0,1:T(1,128)}), s32[1,8,1024]{2,0,1:T(1,128)S(1)}, u32[]{:S(2)}, u32[]{:S(2)}) async-start(s32[1,8,1024]{2,0,1:T(1,128)} %bitcast), calls=%async_computation | async-start | bytes 65536 | tf_op jit(solution)/shard_map/all_to_all | solution.py:94
  83.7 10.8 %all-to-all-start.1 = ((f32[4,8,1024]{2,0,1:T(4,128)}), f32[4,8,1024]{2,0,1:T(4,128)S(1)}, u32[]{:S(2)}, u32[]{:S(2)}) async-start(f32[4,8,1024]{2,0,1:T(4,128)} %copy.405), calls=%async_computation.1 | async-start | bytes 262144 | tf_op jit(solution)/shard_map/all_to_all | solution.py:93
  149.7 4.8 %copy-start = (f32[1,256,32]{2,1,0:T(8,128)S(1)}, f32[1,256,32]{2,1,0:T(8,128)}, u32[]{:S(2)}) copy-start(f32[1,256,32]{2,1,0:T(8,128)} %stack.24) | copy-start | bytes 98308
  184.5 10.2 %collective-permute-start = (f32[1,8,8,1,8,8]{2,1,0,5,4,3:T(8,128)S(1)}, f32[1,8,8,1,8,8]{2,1,0,5,4,3:T(8,128)S(1)}, u32[]{:S(2)}, u32[]{:S(2)}) collective-permute-start(f32[1,8,8,1,8,8]{2,1,0,5,4,3:T(8,128)S(1)} %get-tuple-element.30), channel_id=1, source_target_pairs={{0,8},{8,16},{16,24},{1,9},{9,17},{17,25},{2,10},{10,18},{18,26},{... | collective-permute-start | bytes 49160 | tf_op jit(solution)/shard_map/ppermute | solution.py:19
  188.4 12.2 %collective-permute-start.1 = (f32[1,8,8,1,8,8]{2,1,0,5,4,3:T(8,128)S(1)}, f32[1,8,8,1,8,8]{2,1,0,5,4,3:T(8,128)S(1)}, u32[]{:S(2)}, u32[]{:S(2)}) collective-permute-start(f32[1,8,8,1,8,8]{2,1,0,5,4,3:T(8,128)S(1)} %get-tuple-element.31), channel_id=1, source_target_pairs={{8,0},{16,8},{24,16},{9,1},{17,9},{25,17},{10,2},{18,10},{26,18},{... | collective-permute-start | bytes 49160 | tf_op jit(solution)/shard_map/ppermute | solution.py:22
  202.9 9.4 %collective-permute-start.2 = (f32[4,1,8,8,1,8]{2,1,0,5,4,3:T(1,128)S(1)}, f32[4,1,8,8,1,8]{2,1,0,5,4,3:T(1,128)S(1)}, u32[]{:S(2)}, u32[]{:S(2)}) collective-permute-start(f32[4,1,8,8,1,8]{2,1,0,5,4,3:T(1,128)S(1)} %get-tuple-element.26), channel_id=1, source_target_pairs={{0,1},{1,2},{2,3},{3,4},{4,5},{5,6},{6,7},{8,9},{9,10},{10,11},{11... | collective-permute-start | bytes 24584 | tf_op jit(solution)/shard_map/ppermute | solution.py:19
  207.2 6.3 %collective-permute-start.3 = (f32[4,1,8,8,1,8]{2,1,0,5,4,3:T(1,128)S(1)}, f32[4,1,8,8,1,8]{2,1,0,5,4,3:T(1,128)S(1)}, u32[]{:S(2)}, u32[]{:S(2)}) collective-permute-start(f32[4,1,8,8,1,8]{2,1,0,5,4,3:T(1,128)S(1)} %get-tuple-element.27), channel_id=1, source_target_pairs={{1,0},{2,1},{3,2},{4,3},{5,4},{6,5},{7,6},{9,8},{10,9},{11,10},{12... | collective-permute-start | bytes 24584 | tf_op jit(solution)/shard_map/ppermute | solution.py:22
